TPU v7x, 128 devices: a whole 4x4x4 slice. The times are simulated.
128 devices in a mesh: occ: 8 (over y, core), vir: 16 (over x, z).
Axes of the slice: x: 4, y: 4, z: 4, core: 2. Of those that a mesh axis runs over, the one named last changes fastest.
Arguments:
- amplitudes: bfloat16 [32, 32, 256, 256], P('vir', None, 'occ'), may hold values from -0.0234375 to 0.0234375
- pair_factor: bfloat16 [256, 256, 512], P('vir', 'occ'), may hold values from -1.296875 to 1.296875
- block_factor: bfloat16 [32, 256, 512], P(None, None, ('occ', 'vir')), may hold values from -1.296875 to 1.296875
- cycle_matrix: bfloat16 [8192, 8192], P('occ', 'vir'), may hold values from -0.0625 to 0.0625
- occ_energy: float32 [32], replicated, may hold values from -2 to -0.3
- block_energy: float32 [32], replicated, may hold values from 0.2 to 3
- virt_energy: float32 [256], replicated, may hold values from 0.2 to 3
Outputs:
- update: float32 [1024, 8192], P('occ', 'vir')
All inputs are finite; a program needn't handle non-finite values.
Results may differ from a plain program's by a relative error of at most 0.0035.
Values may be sent and summed in bfloat16 or wider, within the bound.
No kernel may reach another device: no remote copies, remote signals or barrier semaphores. Data moves between devices by JAX's collectives and lax.ppermute only.
A program may use at most 128 MiB of HBM per device.

v0:
```python
import jax
import jax.numpy as jnp
from jax import lax
from jax.sharding import PartitionSpec as P


def cut_along(value, dim, peers):
    dims = value.shape
    pieces = value.reshape(*dims[:dim], peers, dims[dim] // peers, *dims[dim + 1 :])
    return jnp.moveaxis(pieces, dim, 0)


def sent_and_summed(value, axis, dim):
    peers = lax.axis_size(axis)
    pieces = lax.all_to_all(cut_along(value, dim, peers), axis, 0, 0, tiled=True)
    return jnp.sum(pieces, axis=0)


def copy_for_each(value, axis):
    peers = lax.axis_size(axis)
    return lax.all_to_all(
        jnp.broadcast_to(value[None], (peers, *value.shape)), axis, 0, 0, tiled=True
    )


def joined_along(pieces, dim):
    pieces = jnp.moveaxis(pieces, 0, dim)
    dims = pieces.shape
    return pieces.reshape(*dims[:dim], dims[dim] * dims[dim + 1], *dims[dim + 2 :])


def gathered_copies(value, axis, dim):
    pieces = copy_for_each(value, axis)
    return joined_along(pieces, dim)


def form_integrals(factor_rows, local_rows):
    return lax.dot_general(
        factor_rows, local_rows, (((1,), (1,)), ((), ())), preferred_element_type=jnp.float32
    ).astype(jnp.bfloat16)


def on_device(
    amplitudes, pair_factor, block_factor, cycle_matrix, occ_energy, block_energy, virt_energy
):
    factors = lax.all_gather(block_factor, ("occ", "vir"), axis=2, tiled=True)
    vblock, nvirt, naux = factors.shape
    pair_first, pair_second = (pair_factor.shape[0], pair_factor.shape[1])
    local_rows = pair_factor.reshape(pair_first * pair_second, naux)
    grouped = factors.reshape(vblock // 8, 8 * nvirt, naux)
    integral = lax.map(lambda rows: form_integrals(rows, local_rows), grouped)
    integral = integral.reshape(vblock, nvirt, pair_first, pair_second)
    partial_value = jnp.einsum(
        "ijdc,acbd->ijab",
        lax.all_gather(amplitudes, "vir", axis=0, tiled=True),
        integral,
        preferred_element_type=jnp.float32,
    )
    ladder = sent_and_summed(partial_value, "occ", 0)
    occ_rows, occ_all = (ladder.shape[0], ladder.shape[1])
    rounded = ladder.astype(jnp.bfloat16)
    columns = gathered_copies(rounded, "vir", 3)
    holes = columns.transpose(0, 2, 1, 3).reshape(occ_rows * vblock, occ_all * nvirt)
    cycle = jnp.dot(
        holes,
        lax.all_gather(cycle_matrix, "occ", axis=0, tiled=True),
        preferred_element_type=jnp.float32,
    )
    pair_cols = ladder.shape[3]
    occ_here = lax.dynamic_slice_in_dim(occ_energy, lax.axis_index("occ") * occ_rows, occ_rows, 0)
    virt_here = lax.dynamic_slice_in_dim(
        virt_energy, lax.axis_index("vir") * pair_cols, pair_cols, 0
    )
    divisor = (
        block_energy[None, :, None, None]
        + virt_here[None, None, :, None]
        - occ_here[:, None, None, None]
        - occ_energy[None, None, None, :]
    )
    residual = ladder.transpose(0, 2, 3, 1).reshape(occ_rows * vblock, pair_cols * occ_all) + cycle
    return residual / divisor.reshape(occ_rows * vblock, pair_cols * occ_all)


def solution(mesh):
    return jax.shard_map(
        on_device,
        mesh=mesh,
        in_specs=(
            P("vir", None, "occ", None),
            P("vir", "occ", None),
            P(None, None, ("occ", "vir")),
            P("occ", "vir"),
            P(),
            P(),
            P(),
        ),
        out_specs=P("occ", "vir"),
        check_vma=False,
    )
```

profile of v0, /device:TPU:0, one launch (start us, length us, event | category | flops | bytes accessed | tf_op | source)
XLA Modules:
  0.0 404.1 jit_solution(9662574010172462724)
XLA Ops:
  6.5 0.0 all-gather.4.cloned.1.call-start
  6.5 1.5 copy.18
  8.0 0.0 all-gather.4.cloned.1.call-update
  8.0 0.0 all-gather.6.cloned.1.call-start
  8.1 0.7 all-gather.6.cloned.1.call-update
  8.8 0.0 all-gather.8.cloned.1.call-start
  8.8 0.7 all-gather.8.cloned.1.call-update
  9.5 0.0 copy-start.3
  9.5 73.2 %all-gather.4.cloned.1.call-done = bf16[32,256,512]{1,0,2:T(8,128)(2,1)} async-done(((bf16[32,256,4]{1,0,2:T(8,128)(2,1)}), bf16[32,256,512]{1,0,2:T(8,128)(2,1)}) %all-gather.4.cloned.1.call-update) | async-done | bytes 8388624 | tf_op jit(solution)/shard_map/all_gather | solution.py:46
  82.7 14.0 %copy.31 = bf16[32,256,512]{2,1,0:T(8,128)(2,1)} copy(bf16[32,256,512]{1,0,2:T(8,128)(2,1)} %all-gather.4.cloned.1.call-done) | data formatting | bytes 16777216 | tf_op jit(solution)/shard_map/while | solution.py:51
  96.7 0.0 copy-done.3
  96.7 17.0 %while.10 = (s32[]{:T(128)}, bf16[4,2048,512]{2,1,0:T(8,128)(2,1)}, bf16[4,2048,512]{2,1,0:T(8,128)(2,1)}, bf16[512,512]{1,0:T(8,128)(2,1)S(1)}, s32[]{:T(128)}) while((s32[]{:T(128)}, bf16[4,2048,512]{2,1,0:T(8,128)(2,1)}, bf16[4,2048,512]{2,1,0:T(8,128)(2,1)}, bf16[512,512]{1,0:T(8,128)(2,1)S(1)}, s32[]{:T(128)}) %tuple.29), condition=%wide.region_1.2_spmd, body=%wide.region_0.1_spmd.sunk | while | flops 1074790400 | bytes 4719677 | solution.py:51
  96.7 4.2 %fusion.18 = bf16[4,2048,512]{2,1,0:T(8,128)(2,1)} fusion(bf16[4,2048,512]{2,1,0:T(8,128)(2,1)} %get-tuple-element.71, s32[]{:T(128)} %get-tuple-element.70, bf16[512,512]{1,0:T(8,128)(2,1)S(1)} %get-tuple-element.78, bf16[4,2048,512]{2,1,0:T(8,128)(2,1)} %get-tuple-element.77), kind=kOutput, calls=%fused_computation.2.clone.1 | convolution fusion | flops 1074790400 | bytes 4719616 | tf_op jit(solution)/shard_map/while/body/eval_jaxpr/dot_general | solution.py:38
  101.0 4.2 %fusion.18 = bf16[4,2048,512]{2,1,0:T(8,128)(2,1)} fusion(bf16[4,2048,512]{2,1,0:T(8,128)(2,1)} %get-tuple-element.71, s32[]{:T(128)} %get-tuple-element.70, bf16[512,512]{1,0:T(8,128)(2,1)S(1)} %get-tuple-element.78, bf16[4,2048,512]{2,1,0:T(8,128)(2,1)} %get-tuple-element.77), kind=kOutput, calls=%fused_computation.2.clone.1 | convolution fusion | flops 1074790400 | bytes 4719616 | tf_op jit(solution)/shard_map/while/body/eval_jaxpr/dot_general | solution.py:38
  105.2 4.3 %fusion.18 = bf16[4,2048,512]{2,1,0:T(8,128)(2,1)} fusion(bf16[4,2048,512]{2,1,0:T(8,128)(2,1)} %get-tuple-element.71, s32[]{:T(128)} %get-tuple-element.70, bf16[512,512]{1,0:T(8,128)(2,1)S(1)} %get-tuple-element.78, bf16[4,2048,512]{2,1,0:T(8,128)(2,1)} %get-tuple-element.77), kind=kOutput, calls=%fused_computation.2.clone.1 | convolution fusion | flops 1074790400 | bytes 4719616 | tf_op jit(solution)/shard_map/while/body/eval_jaxpr/dot_general | solution.py:38
  109.5 4.2 %fusion.18 = bf16[4,2048,512]{2,1,0:T(8,128)(2,1)} fusion(bf16[4,2048,512]{2,1,0:T(8,128)(2,1)} %get-tuple-element.71, s32[]{:T(128)} %get-tuple-element.70, bf16[512,512]{1,0:T(8,128)(2,1)S(1)} %get-tuple-element.78, bf16[4,2048,512]{2,1,0:T(8,128)(2,1)} %get-tuple-element.77), kind=kOutput, calls=%fused_computation.2.clone.1 | convolution fusion | flops 1074790400 | bytes 4719616 | tf_op jit(solution)/shard_map/while/body/eval_jaxpr/dot_general | solution.py:38
  113.7 15.1 %copy.20 = bf16[4,2048,512]{1,0,2:T(4,128)(2,1)} copy(bf16[4,2048,512]{2,1,0:T(8,128)(2,1)} %get-tuple-element.27) | data formatting | bytes 16777216 | tf_op jit(solution)/shard_map/while | solution.py:51
  128.8 14.4 %reshape.71 = bf16[32,256,16,32]{1,0,3,2:T(8,128)(2,1)} reshape(bf16[4,2048,512]{1,0,2:T(4,128)(2,1)} %copy.20) | data formatting | bytes 16777216 | tf_op jit(solution)/shard_map/reshape | solution.py:52
  143.3 50.4 %all-gather.6.cloned.1.call-done = bf16[32,32,32,256]{3,2,1,0:T(8,128)(2,1)} async-done(((bf16[2,32,32,256]{3,2,1,0:T(8,128)(2,1)}), bf16[32,32,32,256]{3,2,1,0:T(8,128)(2,1)}) %all-gather.6.cloned.1.call-update) | async-done | bytes 16777232 | tf_op jit(solution)/shard_map/all_gather | solution.py:55
  193.7 42.8 %fusion.5 = f32[32,16,32,32,1]{3,1,4,2,0:T(8,128)S(1)} fusion(bf16[32,32,32,256]{3,2,1,0:T(8,128)(2,1)} %all-gather.6.cloned.1.call-done, bf16[32,256,16,32,1]{1,0,3,2,4:T(8,128)(2,1)} %bitcast.58), kind=kOutput, calls=%fused_computation.6 | convolution fusion | flops 8589934592 | bytes 27262976 | tf_op jit(solution)/shard_map/ijdc,acbd->ijab/dot_general | solution.py:53
  236.5 4.2 %copy.43 = f32[8,4,32,32,16]{2,4,1,3,0:T(8,128)} copy(f32[8,4,32,32,16]{2,4,1,0,3:T(8,128)S(1)} %bitcast.59) | data formatting | bytes 4194304 | tf_op jit(solution)/shard_map/reshape | solution.py:9
  240.8 7.6 %reshape.79 = f32[8,1,65536]{2,1,0:T(1,128)S(1)} reshape(f32[8,32,4,16,32]{4,3,2,1,0:T(8,128)} %bitcast.52) | data formatting | bytes 4194304
  248.3 31.3 %all_to_all.10 = f32[8,1,65536]{2,1,0:T(1,128)} all-to-all(f32[8,1,65536]{2,1,0:T(1,128)S(1)} %reshape.79), channel_id=1, replica_groups=mesh['occ'=8,'vir'=16] {'occ'}, dimensions={0} | all-to-all | bytes 4194304 | tf_op jit(solution)/shard_map/all_to_all | solution.py:15
  279.6 0.5 broadcast.43
  280.1 7.2 %reduce = f32[8,65536]{1,0:T(8,128)S(1)} reduce(f32[8,1,65536]{2,1,0:T(1,128)} %all_to_all.10, f32[]{:T(128)} %broadcast.43), dimensions={1}, to_apply=%all_to_all.6.reduce_sub_computation | reduce | bytes 4194308 | tf_op jit(solution)/shard_map/all_to_all | solution.py:15
  287.4 6.0 %reshape.80 = f32[8,32,4,16,32]{4,3,2,1,0:T(8,128)} reshape(f32[8,65536]{1,0:T(8,128)S(1)} %reduce) | data formatting | bytes 4194304
  293.3 4.5 %bitcast_reduce_fusion = f32[4,32,32,16]{1,3,0,2:T(8,128)S(1)} fusion(f32[8,32,4,16,32]{4,3,2,1,0:T(8,128)} %reshape.80), kind=kLoop, calls=%fused_computation.15 | loop fusion | flops 458752 | bytes 2359296 | tf_op jit(solution)/shard_map/reduce_sum | solution.py:16
  297.9 0.1 convert_element_type.10
  298.0 0.9 copy.26
  298.9 5.2 %broadcast_bitcast_fusion = bf16[16,4,32,16,32]{4,3,2,1,0:T(8,128)(2,1)} fusion(bf16[4,32,32,16]{2,3,1,0:T(8,128)(2,1)S(1)} %copy.26), kind=kLoop, calls=%fused_computation.17 | loop fusion | bytes 2228224
  304.1 0.0 copy-start.4
  304.1 0.0 copy-start.2
  304.1 0.0 copy-start.1
  304.1 14.5 %reshape.81 = bf16[16,2,32768]{2,1,0:T(2,128)(2,1)} reshape(bf16[16,4,32,16,32]{4,3,2,1,0:T(8,128)(2,1)} %broadcast_bitcast_fusion) | data formatting | bytes 4194304
  318.6 5.3 %all-to-all-start.1 = ((bf16[16,2,32768]{2,1,0:T(2,128)(2,1)}), bf16[16,2,32768]{2,1,0:T(2,128)(2,1)S(1)}, u32[]{:S(2)}, u32[]{:S(2)}) async-start(bf16[16,2,32768]{2,1,0:T(2,128)(2,1)} %reshape.81), calls=%async_computation.1 | async-start | bytes 4194304 | tf_op jit(solution)/shard_map/all_to_all | solution.py:21
  323.9 0.0 copy-done.4
  323.9 0.1 dynamic_slice.10
  324.0 0.0 copy-done.2
  324.0 0.1 dynamic_slice.11
  324.0 0.0 copy-done.1
  324.0 0.1 broadcast_add_fusion
  324.1 0.1 broadcast_subtract_fusion
  324.2 1.3 sub.41
  325.5 1.6 sub.42
  327.2 0.1 sub.44
  327.2 1.1 copy.25
  328.3 2.3 reshape.73
  330.6 23.0 %all-to-all-done.1 = bf16[16,2,32768]{2,1,0:T(2,128)(2,1)S(1)} async-done(((bf16[16,2,32768]{2,1,0:T(2,128)(2,1)}), bf16[16,2,32768]{2,1,0:T(2,128)(2,1)S(1)}, u32[]{:S(2)}, u32[]{:S(2)}) %all-to-all-start.1) | async-done | bytes 2097184 | tf_op jit(solution)/shard_map/all_to_all | solution.py:21
  353.6 8.8 %reshape.82 = bf16[16,4,32,16,32]{4,3,2,1,0:T(8,128)(2,1)} reshape(bf16[16,2,32768]{2,1,0:T(2,128)(2,1)S(1)} %all-to-all-done.1) | data formatting | bytes 4194304
  362.3 9.3 %bitcast_bitcast_fusion = bf16[4,32,32,16,16]{2,4,1,0,3:T(8,128)(2,1)} fusion(bf16[16,4,32,16,32]{4,3,2,1,0:T(8,128)(2,1)} %reshape.82), kind=kLoop, calls=%fused_computation.14 | loop fusion | bytes 4194304 | tf_op jit(solution)/shard_map/transpose | solution.py:27
  371.6 9.0 %copy.27 = bf16[4,32,32,16,16]{2,4,3,1,0:T(8,128)(2,1)} copy(bf16[4,32,32,16,16]{2,4,1,0,3:T(8,128)(2,1)} %bitcast_bitcast_fusion) | data formatting | bytes 4194304 | tf_op jit(solution)/shard_map/transpose | solution.py:27
  380.6 0.0 copy-start
  380.6 8.6 %copy.28 = bf16[4,32,32,256]{3,2,1,0:T(8,128)(2,1)} copy(bf16[4,32,32,256]{1,3,2,0:T(8,128)(2,1)} %bitcast.53) | data formatting | bytes 4194304 | tf_op jit(solution)/shard_map/transpose | solution.py:63
  389.2 3.0 copy.35
  392.2 0.0 all-gather.8.cloned.1.call-done
  392.3 0.0 copy-done
  392.3 5.4 %fusion.9 = f32[128,512]{1,0:T(8,128)} fusion(f32[128,512]{1,0:T(8,128)S(1)} %copy-done, bf16[128,8192]{1,0:T(8,128)(2,1)S(1)} %bitcast.54, bf16[8192,512]{1,0:T(8,128)(2,1)} %all-gather.8.cloned.1.call-done, f32[128,512]{1,0:T(8,128)S(1)} %sub.42, f32[512]{0:T(512)S(1)} %sub.44), kind=kOutput, calls=%fused_computation.11 | convolution fusion | flops 1073938432 | bytes 11274240 | tf_op jit(solution)/shard_map/dot_general | solution.py:64
  (2 shorter events, 0.0 us)
Async XLA Ops:
  6.5 76.2 %all-gather.4.cloned.1.call-start = ((), (), s32[]{:S(2)}) async-start(), calls=%async_computation.2 | async-start | bytes 8454144 | tf_op jit(solution)/shard_map/all_gather | solution.py:46
  8.0 185.7 %all-gather.6.cloned.1.call-start = ((), (), s32[]{:S(2)}) async-start(), calls=%async_computation.3 | async-start | bytes 17825792 | tf_op jit(solution)/shard_map/all_gather | solution.py:55
  8.8 383.5 %all-gather.8.cloned.1.call-start = ((), (), s32[]{:S(2)}) async-start(), calls=%async_computation.4 | async-start | bytes 9437184 | tf_op jit(solution)/shard_map/all_gather | solution.py:66
  9.5 87.2 %copy-start.3 = (bf16[16,32,512]{2,1,0:T(8,128)(2,1)S(1)}, bf16[16,32,512]{2,1,0:T(8,128)(2,1)}, u32[]{:S(2)}) copy-start(bf16[16,32,512]{2,1,0:T(8,128)(2,1)} %param.10) | copy-start | bytes 1572868
  304.1 19.8 %copy-start.4 = (f32[256]{0:T(256)S(1)}, f32[256]{0:T(256)}, u32[]{:S(2)}) copy-start(f32[256]{0:T(256)} %param.15) | copy-start | bytes 3076
  304.1 19.9 %copy-start.2 = (f32[32]{0:T(128)S(1)}, f32[32]{0:T(128)}, u32[]{:S(2)}) copy-start(f32[32]{0:T(128)} %param.13) | copy-start | bytes 388
  304.1 19.9 %copy-start.1 = (f32[32]{0:T(128)S(1)}, f32[32]{0:T(128)}, u32[]{:S(2)}) copy-start(f32[32]{0:T(128)} %param.14) | copy-start | bytes 388
  318.6 35.0 %all-to-all-start.1 = ((bf16[16,2,32768]{2,1,0:T(2,128)(2,1)}), bf16[16,2,32768]{2,1,0:T(2,128)(2,1)S(1)}, u32[]{:S(2)}, u32[]{:S(2)}) async-start(bf16[16,2,32768]{2,1,0:T(2,128)(2,1)} %reshape.81), calls=%async_computation.1 | async-start | bytes 4194304 | tf_op jit(solution)/shard_map/all_to_all | solution.py:21
  380.6 11.6 %copy-start = (f32[128,512]{1,0:T(8,128)S(1)}, f32[128,512]{1,0:T(8,128)}, u32[]{:S(2)}) copy-start(f32[128,512]{1,0:T(8,128)} %reshape.73) | copy-start | bytes 786436
Sparse Core Ops, SparseCore 0:
  10.5 72.1 all-gather.3
  84.9 108.8 all-gather.5
  195.4 49.2 all-gather.7
where the time goes:
time: 406 us; the launch traced here: 404 us
  waiting for transfers between devices  148 us (36%)
  local copies, waits for them, and re-layouts  129 us (32%)
  matrix products  65.2 us (16%)
  blocking collectives  31.3 us (8%)
  between operations  13.2 us (3%)
  other arithmetic  12 us (3%)
  starting transfers between devices  5.34 us (1%)
    all_gather x1, waiting for transfers between devices, on_device(): factors = lax.all_gather(block_factor, ('occ', 'vir'), axis=2, tiled=True)  73.2 us
    all_gather x1, waiting for transfers between devices, on_device(): lax.all_gather(amplitudes, 'vir', axis=0, tiled=True)  50.4 us
    unnamed x17, local copies, waits for them, and re-layouts  46.5 us
    dot_general x1, matrix products, on_device(): jnp.einsum('ijdc,acbd->ijab', lax.all_gather(amplitudes, 'vir', axis=0, t...  42.8 us
    all_to_all x1, blocking collectives, sent_and_summed(): lax.all_to_all(cut_along(value, dim, peers), axis, 0, 0, tiled=True)  31.3 us
    while x2, local copies, waits for them, and re-layouts, on_device(): integral = lax.map(lambda rows: form_integrals(rows, local_rows), grouped)  29.1 us
    all_to_all x1, waiting for transfers between devices, copy_for_each(): lax.all_to_all(jnp.broadcast_to(value[None], (peers, *value.shape)), axis...  23 us
    transpose x2, local copies, waits for them, and re-layouts, joined_along(): pieces = jnp.moveaxis(pieces, 0, dim)  18.3 us
  transfers between devices with their start and end apart: 4, of which 3 were waited for; matrix products, arithmetic and copies ran while one was open for 49% of the time, Pallas kernels for 0%

commit v1 on v0

v1 whole, which is shorter than its diff:
```python
import functools

import jax
import jax.numpy as jnp
from jax import lax
from jax.experimental import pallas as pl
from jax.experimental.pallas import tpu as pltpu
from jax.sharding import PartitionSpec as P

BF16, F32 = jnp.bfloat16, jnp.float32
OCC, VIR = ("y", "core"), ("x", "z")
ALL_CZ = [(c, z) for c in range(2) for z in range(4)]


def amplitude_route(alpha):
    return [(c * 4 + z, (z // 2) * 4 + 2 * c + ((z % 2) ^ alpha)) for c, z in ALL_CZ]


def factor_route(gamma):
    return [(c * 4 + z, ((z ^ gamma) // 2) * 4 + 2 * c + ((z ^ gamma) % 2)) for c, z in ALL_CZ]


def integrals_kernel(where_ref, pair_ref, block_ref, out_ref):
    slots, nd, nb, naux = pair_ref.shape
    nc = block_ref.shape[3]
    rhs = jnp.concatenate(
        [block_ref[:, k].reshape(naux, nc) for k in range(block_ref.shape[1])], axis=1
    )
    for s in range(slots):
        lhs = pair_ref[where_ref[0] ^ s].reshape(nd * nb, naux)
        got = jnp.dot(lhs, rhs, preferred_element_type=F32).astype(BF16)
        for k in range(block_ref.shape[1]):
            for d in range(nd):
                out_ref[
                    (k * slots + s) * nb : (k * slots + s + 1) * nb, d * nc : (d + 1) * nc
                ] = got[d * nb : (d + 1) * nb, k * nc : (k + 1) * nc]


def form_integrals(where, pair, block):
    slots, nd, nb, naux = pair.shape
    groups, na, nq, nc = block.shape
    step = 2
    return pl.pallas_call(
        integrals_kernel,
        grid_spec=pltpu.PrefetchScalarGridSpec(
            num_scalar_prefetch=1,
            grid=(na // step,),
            in_specs=[
                pl.BlockSpec((slots, nd, nb, naux), lambda g, w: (0, 0, 0, 0)),
                pl.BlockSpec((groups, step, nq, nc), lambda g, w: (0, g, 0, 0)),
            ],
            out_specs=pl.BlockSpec((step * slots * nb, nd * nc), lambda g, w: (g, 0)),
        ),
        out_shape=jax.ShapeDtypeStruct((na * slots * nb, nd * nc), BF16),
        name="integrals",
    )(where, pair, block)


def ladder_kernel(half_ref, amp_ref, w_ref, out_ref, turned):
    nx, two, nd, rows, nc = amp_ref.shape
    wide = two * rows

    @pl.when(pl.program_id(0) == 0)
    def _():
        for x in range(nx):
            for d in range(nd):
                pair = jnp.concatenate(
                    [amp_ref[x, half_ref[0] ^ p, d] for p in range(two)], axis=0
                )
                turned[d * nc : (d + 1) * nc, x * wide : (x + 1) * wide] = pair.T

    got = jnp.dot(w_ref[...], turned[...], preferred_element_type=F32).astype(BF16)
    ny, nz, na, nb, _ = out_ref.shape
    for y in range(ny):
        for z in range(nz):
            for a in range(na):
                row = (a * nz + z) * nb
                out_ref[y, z, a] = got[row : row + nb, y * wide : (y + 1) * wide]


def partial_ladder(half, amp, w, nz):
    nx, two, nd, rows, nc = amp.shape
    nrow, depth = w.shape
    step = 512
    nb = 16
    na = step // (nz * nb)
    return pl.pallas_call(
        ladder_kernel,
        grid_spec=pltpu.PrefetchScalarGridSpec(
            num_scalar_prefetch=1,
            grid=(nrow // step,),
            in_specs=[
                pl.BlockSpec(amp.shape, lambda g, h: (0, 0, 0, 0, 0)),
                pl.BlockSpec((step, depth), lambda g, h: (g, 0)),
            ],
            out_specs=pl.BlockSpec((nx, nz, na, nb, two * rows), lambda g, h: (0, 0, g, 0, 0)),
            scratch_shapes=[pltpu.VMEM((depth, nx * two * rows), BF16)],
        ),
        out_shape=jax.ShapeDtypeStruct((nx, nz, nrow // (nz * nb), nb, two * rows), BF16),
        name="ladder",
    )(half, amp, w)


def settle_kernel(parts_ref, direct_ref, holes_ref, total, swapped):
    peers, rows, wide = parts_ref.shape
    nb = 16
    na = rows // nb
    ni = wide // na
    nj = wide // ni
    acc = parts_ref[0].astype(F32)
    for p in range(1, peers):
        acc = acc + parts_ref[p].astype(F32)
    total[...] = acc
    per = wide // nj
    for group in range(nb // per):
        blocks = [total[pl.ds(group * per + k, na, stride=nb), :] for k in range(per)]
        for i in range(ni):
            direct_ref[i * na : (i + 1) * na, group * wide : (group + 1) * wide] = jnp.concatenate(
                [m[:, i * nj : (i + 1) * nj] for m in blocks], axis=1
            )
        for k, m in enumerate(blocks):
            flipped = m.T
            swapped[pl.ds(group * per + k, nj, stride=nb), :] = jnp.concatenate(
                [flipped[i * nj : (i + 1) * nj, :] for i in range(ni)], axis=1
            )
    holes_ref[...] = swapped[...].astype(BF16)


def settle(parts):
    peers, rows, wide = parts.shape
    return pl.pallas_call(
        settle_kernel,
        out_shape=(
            jax.ShapeDtypeStruct((128, 512), F32),
            jax.ShapeDtypeStruct((rows, wide), BF16),
        ),
        scratch_shapes=[pltpu.VMEM((rows, wide), F32), pltpu.VMEM((rows, wide), F32)],
        name="settle",
    )(parts)


def cycle_kernel(holes_ref, matrix_ref, direct_ref, row_ref, col_ref, out_ref, acc):
    g = pl.program_id(0)
    peers, nk, nb, wide = holes_ref.shape
    lhs = jnp.concatenate(
        [holes_ref[:, k].reshape(peers * nb, wide).T for k in range(nk)], axis=1
    )
    got = jnp.dot(lhs, matrix_ref[...], preferred_element_type=F32)

    @pl.when(g == 0)
    def _():
        acc[...] = direct_ref[...] + got

    @pl.when(g > 0)
    def _():
        acc[...] += got

    @pl.when(g == pl.num_programs(0) - 1)
    def _():
        out_ref[...] = acc[...] / (row_ref[...] + col_ref[...])


def finish(holes, matrix, direct, row, col):
    peers, nk, nb, wide = holes.shape
    depth, ncol = matrix.shape
    step = 4
    return pl.pallas_call(
        cycle_kernel,
        grid=(nk // step,),
        in_specs=[
            pl.BlockSpec((peers, step, nb, wide), lambda g: (0, g, 0, 0)),
            pl.BlockSpec((step * depth // nk, ncol), lambda g: (g, 0)),
            pl.BlockSpec(direct.shape, lambda g: (0, 0)),
            pl.BlockSpec(row.shape, lambda g: (0, 0)),
            pl.BlockSpec(col.shape, lambda g: (0, 0)),
        ],
        out_specs=pl.BlockSpec(direct.shape, lambda g: (0, 0)),
        out_shape=jax.ShapeDtypeStruct(direct.shape, F32),
        scratch_shapes=[pltpu.VMEM(direct.shape, F32)],
        name="cycle",
    )(holes, matrix, direct, row, col)


def on_device(
    amplitudes, pair_factor, block_factor, cycle_matrix, occ_energy, block_energy, virt_energy
):
    y, core, x, z = (lax.axis_index(n) for n in ("y", "core", "x", "z"))
    half = z % 2
    ni, nj, nd, nc = amplitudes.shape
    pieces = amplitudes.reshape(ni * nj, nd, 2, nc // 2).transpose(2, 1, 0, 3)
    got = [
        lax.ppermute(
            lax.dynamic_index_in_dim(pieces, half ^ alpha, 0, keepdims=False),
            ("core", "z"),
            amplitude_route(alpha),
        )
        for alpha in range(2)
    ]
    amp = lax.all_gather(jnp.stack(got), "x", axis=0)

    turned = pair_factor.transpose(1, 0, 2)
    pair = jnp.stack([lax.ppermute(turned, ("core", "z"), factor_route(g)) for g in range(4)])

    block = lax.all_gather(block_factor.transpose(2, 0, 1), VIR, axis=0)
    nv, nq, na, _ = block.shape
    block = lax.dynamic_slice_in_dim(block, half * (nc // 2), nc // 2, 3)
    block = block.reshape(nv * nq, na, nc // 2).transpose(1, 0, 2)
    block = lax.all_gather(block, OCC, axis=0)

    where = (2 * core + half).astype(jnp.int32).reshape(1)
    w = form_integrals(where, pair, block)
    parts = partial_ladder(half.astype(jnp.int32).reshape(1), amp, w, 4)
    parts = parts.reshape(16, *parts.shape[2:])
    parts = lax.all_to_all(parts, ("y", "z"), 0, 0, tiled=True)
    direct, holes = settle(parts.reshape(16, -1, parts.shape[-1]))
    holes = lax.all_gather(holes.reshape(nj, -1, holes.shape[1]), VIR, axis=0)
    matrix = lax.all_gather(cycle_matrix, OCC, axis=0, tiled=True)

    occ_rows = nj // 8
    cols = virt_energy.shape[0] // 16
    occ_here = lax.dynamic_slice_in_dim(occ_energy, (2 * y + core) * occ_rows, occ_rows, 0)
    virt_here = lax.dynamic_slice_in_dim(virt_energy, (4 * x + z) * cols, cols, 0)
    row = (block_energy[None, :] - occ_here[:, None]).reshape(-1, 1)
    col = (virt_here[:, None] - occ_energy[None, :]).reshape(1, -1)
    return finish(holes, matrix, direct, row, col)


def solution(mesh):
    fine = jax.sharding.Mesh(mesh.devices.reshape(4, 2, 4, 4), ("y", "core", "x", "z"))
    return jax.shard_map(
        on_device,
        mesh=fine,
        in_specs=(
            P(VIR, None, OCC, None),
            P(VIR, OCC, None),
            P(None, None, OCC + VIR),
            P(OCC, VIR),
            P(),
            P(),
            P(),
        ),
        out_specs=P(OCC, VIR),
        check_vma=False,
    )
```

time: 406 us -> 275 us (0.68)
  local copies, waits for them, and re-layouts: 129 us -> 9.85 us
  matrix products: 65.2 us -> 0 us
  Pallas kernels: 0 us -> 44.5 us
  blocking collectives: 31.3 us -> 56.5 us
  waiting for transfers between devices: 148 us -> 136 us
  other arithmetic: 12 us -> 2.77 us
  starting transfers between devices: 5.34 us -> 10.9 us
    dot_general x6 -> x0, matrix products: 65.2 us -> none  [the longest x1 42.8 us: on_device(): jnp.einsum('ijdc,acbd->ijab', lax.all_gather(amplitudes, 'vir', axis=0, t...]
    unnamed x17 -> x12, local copies, waits for them, and re-layouts: 46.5 us -> 1.88 us
    pallas_call x0 -> x4, Pallas kernels: none -> 44.5 us  [the longest x1 17.8 us: form_integrals(): pl.pallas_call(integrals_kernel, grid_spec=pltpu.PrefetchScalarGridSpec(n...]
    ppermute x0 -> x6, waiting for transfers between devices: none -> 36.7 us  [the longest x4 24.2 us: on_device(): lax.ppermute(turned, ('core', 'z'), factor_route(g))]
    while x2 -> x0, local copies, waits for them, and re-layouts: 29.1 us -> none  [on_device(): integral = lax.map(lambda rows: form_integrals(rows, local_rows), grouped)]
    transpose x4 -> x0, local copies, waits for them, and re-layouts: 28 us -> none  [the longest x2 18.3 us: joined_along(): pieces = jnp.moveaxis(pieces, 0, dim)]
    all_to_all x1, blocking collectives: 31.3 us -> 56.5 us  [on_device(): parts = lax.all_to_all(parts, ('y', 'z'), 0, 0, tiled=True)]
    all_gather x3 -> x5, waiting for transfers between devices: 124 us -> 99.2 us  [the longest x1 46.4 us: on_device(): block = lax.all_gather(block_factor.transpose(2, 0, 1), VIR, axis=0)]
  transfers between devices with their start and end apart: 4 -> 11, of which waited for: 3 -> 7; matrix products, arithmetic and copies ran while one was open for 49% -> 3% of each run, Pallas kernels for 0% -> 13%
where the time goes in v1:
time: 275 us; the launch traced here: 274 us
  waiting for transfers between devices  136 us (49%)
  blocking collectives  56.5 us (21%)
  Pallas kernels  44.5 us (16%)
  between operations  13.3 us (5%)
  starting transfers between devices  10.9 us (4%)
  local copies, waits for them, and re-layouts  9.85 us (4%)
  other arithmetic  2.77 us (1%)
    all_to_all x1, blocking collectives, on_device(): parts = lax.all_to_all(parts, ('y', 'z'), 0, 0, tiled=True)  56.5 us
    all_gather x1, waiting for transfers between devices, on_device(): block = lax.all_gather(block_factor.transpose(2, 0, 1), VIR, axis=0)  46.4 us
    all_gather x1, waiting for transfers between devices, on_device(): holes = lax.all_gather(holes.reshape(nj, -1, holes.shape[1]), VIR, axis=0)  44.7 us
    ppermute x4, waiting for transfers between devices, on_device(): lax.ppermute(turned, ('core', 'z'), factor_route(g))  24.2 us
    pallas_call x1, Pallas kernels, form_integrals(): pl.pallas_call(integrals_kernel, grid_spec=pltpu.PrefetchScalarGridSpec(n...  17.8 us
    pallas_call x1, Pallas kernels, partial_ladder(): pl.pallas_call(ladder_kernel, grid_spec=pltpu.PrefetchScalarGridSpec(num_...  15.1 us
    ppermute x2, waiting for transfers between devices, on_device(): lax.ppermute(lax.dynamic_index_in_dim(pieces, half ^ alpha, 0, keepdims=F...  12.5 us
    ppermute x4, starting transfers between devices, on_device(): lax.ppermute(turned, ('core', 'z'), factor_route(g))  8.76 us
  transfers between devices with their start and end apart: 11, of which 7 were waited for; matrix products, arithmetic and copies ran while one was open for 3% of the time, Pallas kernels for 13%

profile of v1, /device:TPU:0, one launch (start us, length us, event | category | flops | bytes accessed | tf_op | source)
XLA Modules:
  0.0 274.2 jit_solution(14090809153926122825)
XLA Ops:
  6.5 0.0 copy-start
  6.5 0.0 all-gather.15.cloned.1.call-start
  6.5 1.6 copy.42
  8.1 0.0 all-gather.15.cloned.1.call-update
  8.1 0.0 all-gather.17.cloned.1.call-start
  8.2 46.4 %all-gather.15.cloned.1.call-done = bf16[64,32,256]{2,1,0:T(8,128)(2,1)} async-done(((bf16[4,32,256]{2,1,0:T(8,128)(2,1)}), bf16[64,32,256]{2,1,0:T(8,128)(2,1)}) %all-gather.15.cloned.1.call-update) | async-done | bytes 1048592 | tf_op jit(solution)/shard_map/all_gather | solution.py:204
  54.6 1.1 constant_dynamic-slice_fusion
  55.7 1.1 copy.33
  56.8 0.0 all-gather.17.cloned.1.call-update
  56.8 0.0 all-gather.13.cloned.1.call-start
  56.9 0.0 copy-done
  56.9 0.3 reshape.69
  57.2 2.7 dynamic-slice_bitcast_fusion.1
  59.9 0.6 copy.41
  60.6 0.7 collective-permute-start
  61.3 0.6 copy.40
  61.9 1.3 collective-permute-start.1
  63.2 0.0 collective-permute-done
  63.2 12.5 %collective-permute-done.1 = bf16[32,64,128]{2,1,0:T(8,128)(2,1)S(1)} collective-permute-done((bf16[32,64,128]{2,1,0:T(8,128)(2,1)S(1)}, bf16[32,64,128]{2,1,0:T(8,128)(2,1)S(1)}, u32[]{:S(2)}, u32[]{:S(2)}) %collective-permute-start.1) | collective-permute-done | bytes 524320 | tf_op jit(solution)/shard_map/ppermute | solution.py:192
  75.6 0.0 copy-start.1
  75.6 1.1 pad_maximum_fusion.1
  76.7 0.0 all-gather.13.cloned.1.call-update
  76.7 0.0 all-gather.11.cloned.1.call-start
  76.8 0.5 all-gather.11.cloned.1.call-update
  77.3 0.0 all-gather.9.cloned.1.call-start
  77.4 0.0 copy-done.1
  77.4 0.3 copy.39
  77.7 0.7 collective-permute-start.2
  78.4 1.4 collective-permute-start.3
  79.8 6.6 %collective-permute-start.4 = (bf16[32,16,512]{2,1,0:T(8,128)(2,1)S(1)}, bf16[32,16,512]{2,1,0:T(8,128)(2,1)S(1)}, u32[]{:S(2)}, u32[]{:S(2)}) collective-permute-start(bf16[32,16,512]{2,1,0:T(8,128)(2,1)S(1)} %bitcast.44), channel_id=1, source_target_pairs={{0,16},{1,17},{2,0},{3,1},{16,18},{17,19},{18,2},{19,3},{4,20},{5,... | collective-permute-start | bytes 1572872 | tf_op jit(solution)/shard_map/ppermute | solution.py:202
  86.4 0.1 collective-permute-start.5
  86.4 0.0 collective-permute-done.2
  86.4 2.3 collective-permute-done.3
  88.7 16.3 %collective-permute-done.4 = bf16[32,16,512]{2,1,0:T(8,128)(2,1)S(1)} collective-permute-done((bf16[32,16,512]{2,1,0:T(8,128)(2,1)S(1)}, bf16[32,16,512]{2,1,0:T(8,128)(2,1)S(1)}, u32[]{:S(2)}, u32[]{:S(2)}) %collective-permute-start.4) | collective-permute-done | bytes 524320 | tf_op jit(solution)/shard_map/ppermute | solution.py:202
  105.0 5.6 %collective-permute-done.5 = bf16[32,16,512]{2,1,0:T(8,128)(2,1)S(1)} collective-permute-done((bf16[32,16,512]{2,1,0:T(8,128)(2,1)S(1)}, bf16[32,16,512]{2,1,0:T(8,128)(2,1)S(1)}, u32[]{:S(2)}, u32[]{:S(2)}) %collective-permute-start.5) | collective-permute-done | bytes 524320 | tf_op jit(solution)/shard_map/ppermute | solution.py:202
  110.7 1.6 pad_maximum_fusion.pair_ref
  112.2 0.0 all-gather.17.cloned.1.call-done
  112.2 17.8 %integrals.1.w_ref = bf16[2048,4096]{1,0:T(8,128)(2,1)} custom-call(s32[1]{0:T(128)} %bitcast.8.where_ref, bf16[4,32,16,512]{3,2,1,0:T(8,128)(2,1)} %pad_maximum_fusion.pair_ref, bf16[8,32,64,128]{3,2,1,0:T(8,128)(2,1)} %bitcast.37), custom_call_target="tpu_custom_call" | custom-call | tf_op jit(solution)/shard_map/integrals/pallas_call | solution.py:43
  130.0 8.1 %all-gather.13.cloned.1.call-done = bf16[8,32,64,128]{3,2,1,0:T(8,128)(2,1)} async-done(((bf16[2,32,64,128]{3,2,1,0:T(8,128)(2,1)}), bf16[8,32,64,128]{3,2,1,0:T(8,128)(2,1)}) %all-gather.13.cloned.1.call-update) | async-done | bytes 4194320 | tf_op jit(solution)/shard_map/all_gather | solution.py:199
  138.1 15.1 %ladder.1 = bf16[4,4,32,16,128]{4,3,2,1,0:T(8,128)(2,1)} custom-call(s32[1]{0:T(128)} %bitcast.half_ref, bf16[4,2,32,64,128]{4,3,2,1,0:T(8,128)(2,1)} %bitcast.38, bf16[2048,4096]{1,0:T(8,128)(2,1)} %integrals.1.w_ref), custom_call_target="tpu_custom_call" | custom-call | tf_op jit(solution)/shard_map/ladder/pallas_call | solution.py:87
  153.2 56.5 %all_to_all.5 = bf16[16,32,16,128]{3,2,1,0:T(8,128)(2,1)} all-to-all(bf16[16,32,16,128]{3,2,1,0:T(8,128)(2,1)} %bitcast.35), channel_id=1, replica_groups=mesh['y'=4,'core'=2,'x'=4,'z'=4] {'y','z'}, dimensions={0} | all-to-all | bytes 4194304 | tf_op jit(solution)/shard_map/all_to_all | solution.py:214
  209.7 0.0 copy-start.4
  209.7 0.0 copy-start.2
  209.7 0.0 copy-start.3
  209.7 3.3 %settle.1 = (f32[128,512]{1,0:T(8,128)}, bf16[512,128]{1,0:T(8,128)(2,1)}) custom-call(bf16[16,512,128]{2,1,0:T(8,128)(2,1)} %bitcast.36), custom_call_target="tpu_custom_call" | custom-call | tf_op jit(solution)/shard_map/settle/pallas_call | solution.py:131
  213.0 0.0 all-gather.9.cloned.1.call-update
  213.0 0.0 copy-done.4
  213.0 0.1 dynamic_slice.20
  213.1 0.0 copy-done.2
  213.1 0.1 broadcast_subtract_fusion
  213.2 0.7 sub.53.col_ref
  213.8 0.1 dynamic_slice.19
  213.9 0.0 copy-done.3
  213.9 0.1 broadcast_subtract_fusion.1
  214.0 0.7 sub.54.row_ref
  214.7 0.0 all-gather.11.cloned.1.call-done.matrix_ref
  214.7 44.7 %all-gather.9.cloned.1.call-done.holes_ref = bf16[16,32,16,128]{3,2,1,0:T(8,128)(2,1)} async-done(((bf16[1,32,16,128]{3,2,1,0:T(8,128)(2,1)}), bf16[16,32,16,128]{3,2,1,0:T(8,128)(2,1)}) %all-gather.9.cloned.1.call-update) | async-done | bytes 2097168 | tf_op jit(solution)/shard_map/all_gather | solution.py:216
  259.4 8.3 %cycle.1 = f32[128,512]{1,0:T(8,128)} custom-call(bf16[16,32,16,128]{3,2,1,0:T(8,128)(2,1)} %all-gather.9.cloned.1.call-done.holes_ref, bf16[8192,512]{1,0:T(8,128)(2,1)} %all-gather.11.cloned.1.call-done.matrix_ref, f32[128,512]{1,0:T(8,128)} %get-tuple-element.8.direct_ref, f32[128,1]{1,0:T(8,128)} %sub.54.row_ref, f32[1,512]{1,0:T(1,128)} %sub.53.col_ref), custom_call_target="tpu_custom_call" | custom-call | tf_op jit(solution)/shard_map/cycle/pallas_call | solution.py:167
Async XLA Ops:
  6.5 50.3 %copy-start = (bf16[2,32,32,256]{3,2,1,0:T(8,128)(2,1)S(1)}, bf16[2,32,32,256]{3,2,1,0:T(8,128)(2,1)}, u32[]{:S(2)}) copy-start(bf16[2,32,32,256]{3,2,1,0:T(8,128)(2,1)} %param.7) | copy-start | bytes 3145732
  6.5 48.1 %all-gather.15.cloned.1.call-start = ((), (), s32[]{:S(2)}) async-start(), calls=%async_computation.4 | async-start | bytes 1114112 | tf_op jit(solution)/shard_map/all_gather | solution.py:204
  8.1 104.1 %all-gather.17.cloned.1.call-start = ((), (), s32[]{:S(2)}) async-start(), calls=%async_computation.5 | async-start | bytes 4718592 | tf_op jit(solution)/shard_map/all_gather | solution.py:208
  56.8 81.3 %all-gather.13.cloned.1.call-start = ((), (), s32[]{:S(2)}) async-start(), calls=%async_computation.3 | async-start | bytes 5242880 | tf_op jit(solution)/shard_map/all_gather | solution.py:199
  60.6 2.6 collective-permute-start
  61.9 13.7 %collective-permute-start.1 = (bf16[32,64,128]{2,1,0:T(8,128)(2,1)S(1)}, bf16[32,64,128]{2,1,0:T(8,128)(2,1)S(1)}, u32[]{:S(2)}, u32[]{:S(2)}) collective-permute-start(bf16[32,64,128]{2,1,0:T(8,128)(2,1)S(1)} %bitcast.41), channel_id=1, source_target_pairs={{0,1},{1,0},{2,17},{3,16},{16,3},{17,2},{18,19},{19,18},{4,5},{5,4... | collective-permute-start | bytes 1572872 | tf_op jit(solution)/shard_map/ppermute | solution.py:192
  75.6 1.7 copy-start.1
  76.7 138.0 %all-gather.11.cloned.1.call-start = ((), (), s32[]{:S(2)}) async-start(), calls=%async_computation.2 | async-start | bytes 9437184 | tf_op jit(solution)/shard_map/all_gather | solution.py:217
  77.3 182.1 %all-gather.9.cloned.1.call-start = ((), (), s32[]{:S(2)}) async-start(), calls=%async_computation.1 | async-start | bytes 2228224 | tf_op jit(solution)/shard_map/all_gather | solution.py:216
  77.7 8.8 %collective-permute-start.2 = (bf16[32,16,512]{2,1,0:T(8,128)(2,1)S(1)}, bf16[32,16,512]{2,1,0:T(8,128)(2,1)S(1)}, u32[]{:S(2)}, u32[]{:S(2)}) collective-permute-start(bf16[32,16,512]{2,1,0:T(8,128)(2,1)S(1)} %bitcast.42), channel_id=1, source_target_pairs={{0,0},{1,1},{2,16},{3,17},{16,2},{17,3},{18,18},{19,19},{4,4},{5,5... | collective-permute-start | bytes 1572872 | tf_op jit(solution)/shard_map/ppermute | solution.py:202
  78.4 10.4 %collective-permute-start.3 = (bf16[32,16,512]{2,1,0:T(8,128)(2,1)S(1)}, bf16[32,16,512]{2,1,0:T(8,128)(2,1)S(1)}, u32[]{:S(2)}, u32[]{:S(2)}) collective-permute-start(bf16[32,16,512]{2,1,0:T(8,128)(2,1)S(1)} %bitcast.43), channel_id=1, source_target_pairs={{0,1},{1,0},{2,17},{3,16},{16,3},{17,2},{18,19},{19,18},{4,5},{5,4... | collective-permute-start | bytes 1572872 | tf_op jit(solution)/shard_map/ppermute | solution.py:202
  79.8 25.3 %collective-permute-start.4 = (bf16[32,16,512]{2,1,0:T(8,128)(2,1)S(1)}, bf16[32,16,512]{2,1,0:T(8,128)(2,1)S(1)}, u32[]{:S(2)}, u32[]{:S(2)}) collective-permute-start(bf16[32,16,512]{2,1,0:T(8,128)(2,1)S(1)} %bitcast.44), channel_id=1, source_target_pairs={{0,16},{1,17},{2,0},{3,1},{16,18},{17,19},{18,2},{19,3},{4,20},{5,... | collective-permute-start | bytes 1572872 | tf_op jit(solution)/shard_map/ppermute | solution.py:202
  86.4 24.3 %collective-permute-start.5 = (bf16[32,16,512]{2,1,0:T(8,128)(2,1)S(1)}, bf16[32,16,512]{2,1,0:T(8,128)(2,1)S(1)}, u32[]{:S(2)}, u32[]{:S(2)}) collective-permute-start(bf16[32,16,512]{2,1,0:T(8,128)(2,1)S(1)} %bitcast.45), channel_id=1, source_target_pairs={{0,17},{1,16},{2,1},{3,0},{16,19},{17,18},{18,3},{19,2},{4,21},{5,... | collective-permute-start | bytes 1572872 | tf_op jit(solution)/shard_map/ppermute | solution.py:202
  209.7 3.3 %copy-start.4 = (f32[256]{0:T(256)S(1)}, f32[256]{0:T(256)}, u32[]{:S(2)}) copy-start(f32[256]{0:T(256)} %param.13) | copy-start | bytes 3076
  209.7 3.4 %copy-start.2 = (f32[32]{0:T(128)S(1)}, f32[32]{0:T(128)}, u32[]{:S(2)}) copy-start(f32[32]{0:T(128)} %param.11) | copy-start | bytes 388
  209.7 4.2 %copy-start.3 = (f32[32]{0:T(128)S(1)}, f32[32]{0:T(128)}, u32[]{:S(2)}) copy-start(f32[32]{0:T(128)} %param.12) | copy-start | bytes 388
Sparse Core Ops, SparseCore 0:
  9.5 45.0 all-gather.14
  56.9 31.3 all-gather.16
  90.0 48.0 all-gather.12
  139.7 72.4 all-gather.10
  214.2 45.1 all-gather.8
